TPU v7x, 32 devices: a whole 2x2x4 slice. The times are simulated.
32 devices in a mesh: shuf: 8 (over z, y), rep: 4 (over x, core).
Axes of the slice: x: 2, y: 2, z: 4, core: 2. Of those that a mesh axis runs over, the one named last changes fastest.
Arguments:
- values: bfloat16 [65536, 1024], P('shuf', 'rep')
- subgroup: int32 [512], P('shuf'), may hold values from 0 to 31
- owners: int32 [512, 1], P('shuf'), may hold values from 0 to 7; in each aligned block of 64 rows (0 to 63, 64 to 127, ...) at most 16 rows name the same one
- col_gain: float32 [1024], P('rep'), may hold values from 0.5 to 1.5
- col_bias: float32 [1024], P('rep'), may hold values from -3 to 3
- out_weight: bfloat16 [1024, 1024], P('rep'), may hold values from -0.1875 to 0.1875
Outputs:
- projected: bfloat16 [65536, 1024], P(('shuf', 'rep'))
Inputs may be any that keep to these rules, and one draw needn't show every extreme that they name: `owners`: among the tiles of one index of shuf no owner is named more than 16 times, a bound that some block reaches.
All inputs are finite; a program needn't handle non-finite values.
Results may differ from a plain program's by a relative error of at most 0.015.
Values may be sent and summed in bfloat16 or wider, within the bound.
A program may use at most 64 MiB of HBM per device.

v0:
```python
import functools
import math

import jax
import jax.numpy as jnp
from jax import lax
from jax.experimental import pallas as pl
from jax.experimental.pallas import tpu as pltpu
from jax.sharding import PartitionSpec as P

GRP_DEV = 32
PRIOR = 256
EPS = 1e-05
EXTRA = 8
CHUNKS = 8
FIRST = 5
LOADS = 8
LIMIT = 58900 * 1024
LIMIT_LAST = 8 * 1024 * 1024
MESH = pl.DeviceIdType.MESH


def kernel(
    shuf_size,
    rep_size,
    values,
    weight,
    owner,
    member,
    gain,
    bias,
    out,
    last_scored,
    weights,
    held,
    arrived,
    packets,
    stats_out,
    stats_in,
    scored,
    rep_ready,
    shuf_ready,
    load_sem,
    own_sem,
    val_send,
    val_recv,
    pack_send,
    pack_recv,
    fwd_send,
    fwd_recv,
    wx_send,
    wx_recv,
    wg_send,
    wg_recv,
    wf_send,
    wf_recv,
    wn_send,
    wn_recv,
    st_send,
    st_recv,
):
    shuf, rep = lax.axis_index("shuf"), lax.axis_index("rep")
    half = rep_size // 2
    outer = shuf_size // 2
    slices = weights.shape[2]
    slice_outer = slices // 2
    local_rows, cols = values.shape
    block_rows = local_rows // rep_size
    tiles = member.shape[1]
    tile_rows = local_rows // tiles
    block_tiles = tiles // rep_size
    chunk = block_rows // CHUNKS
    high, low = rep // half, rep % half
    s_out, s_in = shuf // 2, shuf % 2
    mate = s_out * 2 + 1 - s_in
    cut = shuf % slices
    cut_base = shuf - cut
    cut_out = cut // 2

    def rep_peer(dh, dl):
        return ((high + dh) % 2) * half + (low + dl) % half

    def outer_peer(e):
        return ((s_out + e) % outer) * 2 + s_in

    def cut_peer(e):
        return cut_base + ((cut_out + e) % slice_outer) * 2 + s_in

    rep_offsets = [(dh, dl) for dh in range(2) for dl in range(half) if (dh, dl) != (0, 0)]

    def remote(src, dst, send, recv, s, k):
        return pltpu.make_async_remote_copy(
            src_ref=src, dst_ref=dst, send_sem=send, recv_sem=recv,
            device_id=(s, k), device_id_type=MESH,
        )

    def value_copy(dh, dl, ch):
        peer = rep_peer(dh, dl)
        slot = dh * half + dl
        start = pl.multiple_of(peer * block_rows + ch * chunk, chunk)
        return remote(
            values.at[pl.ds(start, chunk)],
            arrived.at[slot, pl.ds(ch * chunk, chunk)],
            val_send.at[slot, ch], val_recv.at[slot, ch], shuf, peer,
        )

    def load_copy(i):
        size = local_rows // LOADS
        return pltpu.make_async_copy(
            values.at[pl.ds(i * size, size)], held.at[pl.ds(i * size, size)], load_sem.at[i]
        )

    own_weight = pltpu.make_async_copy(weight, weights.at[0, 0], own_sem)
    for i in range(LOADS):
        load_copy(i).start()
    own_weight.start()

    barrier = pltpu.get_barrier_semaphore()
    leader, scout = low == 0, low == 1
    for dh, dl in rep_offsets:
        peer = rep_peer(dh, dl)

        @pl.when(peer % half == 0)
        def _():
            pl.semaphore_signal(barrier, inc=1, device_id=(shuf, peer), device_id_type=MESH)

    @pl.when(leader)
    def _():
        pl.semaphore_wait(barrier, rep_size - 1)
        for dl in range(1, half):
            pl.semaphore_signal(
                rep_ready, inc=1, device_id=(shuf, rep_peer(0, dl)), device_id_type=MESH
            )

    @pl.when(jnp.logical_not(leader))
    def _():
        pl.semaphore_wait(rep_ready, 1)

    wx = remote(weight.at[cut], weights.at[1, 0, cut], wx_send, wx_recv, shuf, rep_peer(1, 0))
    wx.start()
    far = [(1, dl) for dl in range(half)]
    near = [(0, dl) for dl in range(1, half)]
    for ch in range(FIRST):
        for dh, dl in far:
            value_copy(dh, dl, ch).start()
    for ch in range(CHUNKS):
        for dh, dl in near:
            value_copy(dh, dl, ch).start()

    shuf_peers = [mate] + [outer_peer(e) for e in range(1, outer)]

    @pl.when(scout)
    def _():
        for s in shuf_peers:
            pl.semaphore_signal(barrier, inc=1, device_id=(s, rep), device_id_type=MESH)
        pl.semaphore_wait(barrier, len(shuf_peers))
        for dl in range(1, half):
            pl.semaphore_signal(
                shuf_ready, inc=1, device_id=(shuf, rep_peer(0, dl)), device_id_type=MESH
            )

    @pl.when(jnp.logical_not(scout))
    def _():
        pl.semaphore_wait(shuf_ready, 1)

    gid_row = (owner[...] * GRP_DEV + member[...]).astype(jnp.float32)
    packets[0, 0, tiles:tiles + 1, :tiles] = gid_row
    square = (tiles, tiles)
    on_diagonal = lax.broadcasted_iota(jnp.int32, square, 0) == lax.broadcasted_iota(jnp.int32, square, 1)
    gid_col = jnp.sum(jnp.where(on_diagonal, gid_row, 0.0), axis=1, keepdims=True)
    gid_col = jnp.concatenate([gid_col, jnp.full((EXTRA, 1), -1.0, jnp.float32)], axis=0)
    group = 8
    per_load = tiles // LOADS
    for i in range(LOADS):
        load_copy(i).wait()

        def sums(g, carry):
            first = pl.multiple_of(i * per_load + g * group, group)
            parts, squares = [], []
            for u in range(group):
                x = held[pl.ds(pl.multiple_of((first + u) * tile_rows, tile_rows), tile_rows), :]
                x = x.astype(jnp.float32)
                parts.append(jnp.sum(x, axis=0, keepdims=True))
                squares.append(jnp.sum(x * x, axis=0, keepdims=True))
            packets[0, 0, pl.ds(first, group), :cols] = jnp.concatenate(parts, axis=0)
            packets[0, 0, pl.ds(first, group), cols:] = jnp.concatenate(squares, axis=0)
            return carry

        lax.fori_loop(0, per_load // group, sums, 0)

    def pack_copy(e):
        return remote(
            packets.at[0, 0], packets.at[0, e], pack_send.at[e], pack_recv.at[e], outer_peer(e), rep
        )

    def fwd_copy(e):
        return remote(
            packets.at[0, e], packets.at[1, e], fwd_send.at[e], fwd_recv.at[e], mate, rep
        )

    def cut_copy(e):
        here = weights.at[1, 0, cut]
        return remote(here, here, wg_send.at[e], wg_recv.at[e], cut_peer(e), rep)

    def cut_forward(e):
        index = ((cut_out + slice_outer - e) % slice_outer) * 2 + s_in
        there = weights.at[1, 0, index]
        return remote(there, there, wf_send.at[e], wf_recv.at[e], mate, rep)

    for e in range(1, outer):
        pack_copy(e).start()
    fwd_copy(0).start()
    wx.wait_recv()
    for e in range(1, slice_outer):
        cut_copy(e).start()

    def members(i, e):
        same = gid_col == packets[i, e, tiles:tiles + 1, :tiles]
        row = lax.broadcasted_iota(jnp.int32, (tiles + EXTRA, tiles), 0)
        return jnp.where(same | (row >= tiles), 1.0, 0.0).astype(jnp.float32)

    def gathered(i, e):
        m = members(i, e)
        part = jnp.dot(
            m, packets[i, e, :tiles, :],
            precision=lax.Precision.HIGHEST, preferred_element_type=jnp.float32,
        )
        return part, jnp.sum(m, axis=1, keepdims=True)

    total, count = gathered(0, 0)
    for e in range(1, outer):
        pack_copy(e).wait_recv()
        fwd_copy(e).start()
        part, number = gathered(0, e)
        total, count = total + part, count + number
    cut_forward(0).start()
    for e in range(1, slice_outer):
        cut_copy(e).wait_recv()
        cut_forward(e).start()
    for e in range(outer):
        fwd_copy(e).wait_recv()
        part, number = gathered(1, e)
        total, count = total + part, count + number

    row_count = float(local_rows * shuf_size)
    overall = total[tiles:tiles + 1] / row_count
    weight_sum = count[:tiles] * float(tile_rows) + float(PRIOR)
    pooled = (total[:tiles] + float(PRIOR) * overall) / weight_sum
    center, second = pooled[:, :cols], pooled[:, cols:]
    scale = lax.rsqrt(second - center * center + EPS) * gain[...]
    offset = bias[...] - center * scale
    for j in range(rep_size):
        stats_out[j, 0] = scale[j * block_tiles:(j + 1) * block_tiles]
        stats_out[j, 1] = offset[j * block_tiles:(j + 1) * block_tiles]

    def stat_copy(dh, dl):
        peer = rep_peer(dh, dl)
        slot = dh * half + dl
        return remote(
            stats_out.at[peer], stats_in.at[slot], st_send.at[slot], st_recv.at[slot], shuf, peer
        )

    for dh, dl in reversed(rep_offsets):
        stat_copy(dh, dl).start()
    for ch in range(FIRST, CHUNKS):
        for dh, dl in far:
            value_copy(dh, dl, ch).start()
    stats_in[0] = stats_out[rep]

    own_weight.wait()
    for e in range(slice_outer):
        cut_forward(e).wait_recv()

    def near_copy(dh, dl):
        return remote(
            weights.at[dh, 0], weights.at[dh, dl],
            wn_send.at[dh, dl], wn_recv.at[dh, dl], shuf, rep_peer(0, dl),
        )

    for dl in range(1, half):
        for dh in range(2):
            near_copy(dh, dl).start()
    for dh, dl in rep_offsets:
        stat_copy(dh, dl).wait_recv()
    for dl in range(1, half):
        for dh in range(2):
            near_copy(dh, dl).wait_recv()

    def score(ch, dst):
        for slot in range(rep_size):
            if slot > 0:
                value_copy(slot // half, slot % half, ch).wait_recv()
            for u in range(chunk // tile_rows):
                tile = ch * (chunk // tile_rows) + u
                at = ch * chunk + u * tile_rows
                if slot == 0:
                    start = pl.multiple_of(rep * block_rows + at, tile_rows)
                    x = held[pl.ds(start, tile_rows), :]
                else:
                    x = arrived[slot, pl.ds(pl.multiple_of(at, tile_rows), tile_rows), :]
                s = stats_in[slot, 0, pl.ds(tile, 1), :]
                t = stats_in[slot, 1, pl.ds(tile, 1), :]
                dst[u * tile_rows:(u + 1) * tile_rows, slot * cols:(slot + 1) * cols] = (
                    x.astype(jnp.float32) * s + t
                ).astype(jnp.bfloat16)

    def project(ch, carry):
        score(ch, scored)
        whole = weights[...].reshape(rep_size * cols, weights.shape[-1])
        out[pl.ds(pl.multiple_of(ch * chunk, chunk), chunk), :] = jnp.dot(
            scored[...], whole, preferred_element_type=jnp.float32
        ).astype(out.dtype)
        return carry

    lax.fori_loop(0, CHUNKS - 1, project, 0)
    score(CHUNKS - 1, last_scored)

    wx.wait_send()
    for ch in range(CHUNKS):
        for dh, dl in rep_offsets:
            value_copy(dh, dl, ch).wait_send()
    for e in range(1, outer):
        pack_copy(e).wait_send()
    for e in range(outer):
        fwd_copy(e).wait_send()
    for e in range(1, slice_outer):
        cut_copy(e).wait_send()
    for e in range(slice_outer):
        cut_forward(e).wait_send()
    for dh, dl in rep_offsets:
        stat_copy(dh, dl).wait_send()
    for dl in range(1, half):
        for dh in range(2):
            near_copy(dh, dl).wait_send()


def finish(early, scored, weights, out, tail, sems):
    rows, last = early.shape[0], scored.shape[0]
    size = rows // (CHUNKS - 1)

    def early_copy(i):
        return pltpu.make_async_copy(
            early.at[pl.ds(i * size, size)], out.at[pl.ds(i * size, size)], sems.at[i]
        )

    for i in range(CHUNKS - 1):
        early_copy(i).start()
    whole = weights[...].reshape(scored.shape[1], weights.shape[-1])
    tail[...] = jnp.dot(scored[...], whole, preferred_element_type=jnp.float32).astype(tail.dtype)
    tail_copy = pltpu.make_async_copy(tail, out.at[pl.ds(rows, last)], sems.at[CHUNKS - 1])
    tail_copy.start()
    for i in range(CHUNKS - 1):
        early_copy(i).wait()
    tail_copy.wait()


def on_device(shuf_size, rep_size, values, subgroup, owners, col_gain, col_bias, out_weight):
    local_rows, cols = values.shape
    tiles = subgroup.shape[0]
    outs = out_weight.shape[1]
    slices = math.gcd(shuf_size, cols // 32)
    outer, half, slice_outer = shuf_size // 2, rep_size // 2, slices // 2
    block_rows = local_rows // rep_size
    chunk = block_rows // CHUNKS
    f32, bf16 = jnp.float32, jnp.bfloat16
    dma = pltpu.SemaphoreType.DMA
    vmem = pl.BlockSpec(memory_space=pltpu.VMEM)
    hbm = pl.BlockSpec(memory_space=pltpu.HBM)
    early, last_scored, weights = pl.pallas_call(
        functools.partial(kernel, shuf_size, rep_size),
        out_shape=(
            pltpu.VMEM((block_rows - chunk, outs), bf16),
            pltpu.VMEM((chunk, rep_size * cols), bf16),
            pltpu.VMEM((2, half, slices, cols // slices, outs), bf16),
        ),
        in_specs=[hbm, hbm, vmem, vmem, vmem, vmem],
        out_specs=(vmem, vmem, vmem),
        scratch_shapes=[
            pltpu.VMEM((local_rows, cols), bf16),
            pltpu.VMEM((rep_size, block_rows, cols), bf16),
            pltpu.VMEM((2, outer, tiles + EXTRA, 2 * cols), f32),
            pltpu.VMEM((rep_size, 2, tiles // rep_size, cols), f32),
            pltpu.VMEM((rep_size, 2, tiles // rep_size, cols), f32),
            pltpu.VMEM((chunk, rep_size * cols), bf16),
            pltpu.SemaphoreType.REGULAR,
            pltpu.SemaphoreType.REGULAR,
            dma((LOADS,)),
            dma,
            dma((rep_size, CHUNKS)),
            dma((rep_size, CHUNKS)),
            dma((outer,)),
            dma((outer,)),
            dma((outer,)),
            dma((outer,)),
            dma,
            dma,
            dma((slice_outer,)),
            dma((slice_outer,)),
            dma((slice_outer,)),
            dma((slice_outer,)),
            dma((2, half)),
            dma((2, half)),
            dma((rep_size,)),
            dma((rep_size,)),
        ],
        compiler_params=pltpu.CompilerParams(
            collective_id=0, has_side_effects=True, vmem_limit_bytes=LIMIT
        ),
    )(
        values,
        out_weight.reshape(slices, cols // slices, outs),
        owners.reshape(1, tiles),
        subgroup.reshape(1, tiles),
        col_gain[None, :],
        col_bias[None, :],
    )
    return pl.pallas_call(
        finish,
        out_shape=jax.ShapeDtypeStruct((block_rows, outs), bf16),
        in_specs=[vmem, vmem, vmem],
        out_specs=hbm,
        scratch_shapes=[pltpu.VMEM((chunk, outs), bf16), dma((CHUNKS,))],
        compiler_params=pltpu.CompilerParams(vmem_limit_bytes=LIMIT_LAST),
    )(early, last_scored, weights)


def solution(mesh):
    return jax.shard_map(
        functools.partial(on_device, mesh.shape["shuf"], mesh.shape["rep"]),
        mesh=mesh,
        in_specs=(P("shuf", "rep"), P("shuf"), P("shuf", None), P("rep"), P("rep"), P("rep", None)),
        out_specs=P(("shuf", "rep"), None),
        check_vma=False,
    )
```

profile of v0, /device:TPU:25, one launch (start us, length us, event | category | flops | bytes accessed | tf_op | source)
XLA Modules:
  0.0 55.4 jit_solution(17236201338272289087)
XLA Ops:
  0.0 53.3 %shard_map.64 = (bf16[1792,1024]{1,0:T(8,128)(2,1)S(1)}, bf16[256,1024]{1,0:T(8,128)(2,1)S(1)}, bf16[2,2,8,32,1024]{4,3,2,1,0:T(8,128)(2,1)S(1)}) custom-call(bf16[8192,256]{1,0:T(8,128)(2,1)} %values.1, bf16[8,32,1024]{2,1,0:T(8,128)(2,1)} %bitcast.5, s32[1,64]{1,0:T(1,128)} %bitcast.8, s32[1,64]{1,0:T(1,128)} %bitcast.9, f32[1,256]{1,0:T(1,128)} %bitcast.6, ...), custom_call_target="tpu_custom_call" | custom-call | tf_op jit(solution)/shard_map/pallas_call | solution.py:369
  53.3 2.1 %shard_map.65 = bf16[2048,1024]{1,0:T(8,128)(2,1)} custom-call(bf16[1792,1024]{1,0:T(8,128)(2,1)S(1)} %get-tuple-element.8.early, bf16[256,1024]{1,0:T(8,128)(2,1)S(1)} %get-tuple-element.9.scored, bf16[2,2,8,32,1024]{4,3,2,1,0:T(8,128)(2,1)S(1)} %get-tuple-element.10.weights), custom_call_target="tpu_custom_call" | custom-call | tf_op jit(solution)/shard_map/pallas_call | solution.py:417
where the time goes:
time: 56.3 us; the launch traced here: 55.4 us
  Pallas kernels  55.4 us (98%)
    pallas_call x1, Pallas kernels, on_device(): pl.pallas_call(functools.partial(kernel, shuf_size, rep_size), out_shape=...  53.3 us
    pallas_call x1, Pallas kernels, on_device(): pl.pallas_call(finish, out_shape=jax.ShapeDtypeStruct((block_rows, outs),...  2.07 us

commit v1 on v0

v1 whole, which is shorter than its diff:
```python
import functools
import math

import jax
import jax.numpy as jnp
from jax import lax
from jax.experimental import pallas as pl
from jax.experimental.pallas import tpu as pltpu
from jax.sharding import PartitionSpec as P

GRP_DEV = 32
PRIOR = 256
EPS = 1e-05
EXTRA = 8
EARLY = 8
PAIR = 2
PARTS = (4, 4, 8)
LIMIT = 58900 * 1024
LIMIT_LAST = 8 * 1024 * 1024
MESH = pl.DeviceIdType.MESH


def kernel(
    shuf_size,
    rep_size,
    early,
    values,
    weight,
    owner,
    member,
    gain,
    bias,
    out,
    last,
    weights,
    held,
    main,
    packets,
    stat,
    stats_in,
    rep_ready,
    shuf_ready,
    load_sem,
    own_sem,
    far_send,
    far_recv,
    near_send,
    near_recv,
    pack_send,
    pack_recv,
    fwd_send,
    fwd_recv,
    wx_send,
    wx_recv,
    wg_send,
    wg_recv,
    wf_send,
    wf_recv,
    wn_send,
    wn_recv,
    st_send,
    st_recv,
):
    shuf, rep = lax.axis_index("shuf"), lax.axis_index("rep")
    half = rep_size // 2
    outer = shuf_size // 2
    slices = weights.shape[2]
    slice_outer = slices // 2
    local_rows, cols = values.shape
    block_rows = local_rows // rep_size
    tiles = member.shape[1]
    tile_rows = local_rows // tiles
    block_tiles = tiles // rep_size
    main_rows = main.shape[0]
    main_tiles = main_rows // tile_rows
    high, low = rep // half, rep % half
    s_out, s_in = shuf // 2, shuf % 2
    mate = s_out * 2 + 1 - s_in
    cut = shuf % slices
    cut_base = shuf - cut
    cut_out = cut // 2

    def rep_peer(dh, dl):
        return ((high + dh) % 2) * half + (low + dl) % half

    def outer_peer(e):
        return ((s_out + e) % outer) * 2 + s_in

    def cut_peer(e):
        return cut_base + ((cut_out + e) % slice_outer) * 2 + s_in

    far = [(1, dl) for dl in range(half)]
    near = [(0, dl) for dl in range(1, half)]
    rep_offsets = near + far

    def remote(src, dst, send, recv, s, k):
        return pltpu.make_async_remote_copy(
            src_ref=src, dst_ref=dst, send_sem=send, recv_sem=recv,
            device_id=(s, k), device_id_type=MESH,
        )

    def held_rows(block, tile, count):
        start = pl.multiple_of((block * block_tiles + tile) * tile_rows, tile_rows)
        return pl.ds(start, count * tile_rows)

    def tile_at(tile):
        if isinstance(tile, int) and tile >= main_tiles:
            return last, pl.ds((tile - main_tiles) * tile_rows, tile_rows)
        return main, pl.ds(pl.multiple_of(tile * tile_rows, tile_rows), tile_rows)

    def slot_cols(dh, dl):
        slot = dh * half + dl
        return pl.ds(slot * cols, cols)

    def far_copy(dl, tile):
        peer = rep_peer(1, dl)
        dst, rows = tile_at(tile)
        return remote(
            held.at[held_rows(peer, tile, 1)], dst.at[rows, slot_cols(1, dl)],
            far_send.at[dl, tile], far_recv.at[dl, tile], shuf, peer,
        )

    def near_copy(dl, part):
        peer = rep_peer(0, dl)
        dst, tile = (main, 0) if part == 0 else (last, main_tiles)
        count = dst.shape[0] // tile_rows
        return remote(
            held.at[held_rows(peer, tile, count)], dst.at[:, slot_cols(0, dl)],
            near_send.at[dl, part], near_recv.at[dl, part], shuf, peer,
        )

    starts = [sum(PARTS[:i]) * block_tiles // sum(PARTS) for i in range(len(PARTS) + 1)]
    order = far + near + [(0, 0)]

    def load_copy(b, i):
        rows = held_rows(rep_peer(*order[b]), starts[i], starts[i + 1] - starts[i])
        return pltpu.make_async_copy(values.at[rows], held.at[rows], load_sem.at[b, i])

    own_weight = pltpu.make_async_copy(weight, weights.at[0, 0], own_sem)
    loads = [(b, i) for i in range(2) for b in range(half)]
    loads += [(b, i) for b in range(rep_size) for i in range(3) if (b, i) not in loads]
    for b, i in loads:
        load_copy(b, i).start()
    own_weight.start()

    barrier = pltpu.get_barrier_semaphore()
    leader, scout = low == half - 1, low == 0
    for dh, dl in rep_offsets:
        peer = rep_peer(dh, dl)

        @pl.when(peer % half == half - 1)
        def _():
            pl.semaphore_signal(barrier, inc=1, device_id=(shuf, peer), device_id_type=MESH)

    @pl.when(leader)
    def _():
        pl.semaphore_wait(barrier, rep_size - 1)
        for dl in range(1, half):
            pl.semaphore_signal(
                rep_ready, inc=1, device_id=(shuf, rep_peer(0, dl)), device_id_type=MESH
            )

    @pl.when(jnp.logical_not(leader))
    def _():
        pl.semaphore_wait(rep_ready, 1)

    waited = set()

    def load_wait(b, i):
        if (b, i) not in waited:
            waited.add((b, i))
            load_copy(b, i).wait()

    wx = remote(weight.at[cut], weights.at[1, 0, cut], wx_send, wx_recv, shuf, rep_peer(1, 0))
    sent = 0
    for i in range(len(PARTS)):
        if sent < early:
            for b in range(half):
                load_wait(b, i)
        while sent < min(early, starts[i + 1]):
            for dh, dl in far:
                far_copy(dl, sent).start()
            sent += 1
            if sent == 1:
                wx.start()

    shuf_peers = [mate] + [outer_peer(e) for e in range(1, outer)]

    @pl.when(scout)
    def _():
        for s in shuf_peers:
            pl.semaphore_signal(barrier, inc=1, device_id=(s, rep), device_id_type=MESH)
        pl.semaphore_wait(barrier, len(shuf_peers))
        for dl in range(1, half):
            pl.semaphore_signal(
                shuf_ready, inc=1, device_id=(shuf, rep_peer(0, dl)), device_id_type=MESH
            )

    @pl.when(jnp.logical_not(scout))
    def _():
        pl.semaphore_wait(shuf_ready, 1)

    gid_row = (owner[...] * GRP_DEV + member[...]).astype(jnp.float32)
    packets[0, 0, tiles:tiles + 1, :tiles] = gid_row
    square = (tiles, tiles)
    on_diagonal = lax.broadcasted_iota(jnp.int32, square, 0) == lax.broadcasted_iota(jnp.int32, square, 1)
    gid_col = jnp.sum(jnp.where(on_diagonal, gid_row, 0.0), axis=1, keepdims=True)
    gid_col = jnp.concatenate([gid_col, jnp.full((EXTRA, 1), -1.0, jnp.float32)], axis=0)
    group = 8
    for b in range(rep_size):
        block = rep_peer(*order[b])
        for g in range(block_tiles // group):
            for i in range(len(PARTS)):
                if starts[i] < (g + 1) * group:
                    load_wait(b, i)
            parts, squares = [], []
            for u in range(group):
                x = held[held_rows(block, g * group + u, 1), :].astype(jnp.float32)
                parts.append(jnp.sum(x, axis=0, keepdims=True))
                squares.append(jnp.sum(x * x, axis=0, keepdims=True))
            first = pl.multiple_of(block * block_tiles + g * group, group)
            packets[0, 0, pl.ds(first, group), :cols] = jnp.concatenate(parts, axis=0)
            packets[0, 0, pl.ds(first, group), cols:] = jnp.concatenate(squares, axis=0)

    def pack_copy(e):
        return remote(
            packets.at[0, 0], packets.at[0, e], pack_send.at[e], pack_recv.at[e], outer_peer(e), rep
        )

    def fwd_copy(e):
        return remote(
            packets.at[0, e], packets.at[1, e], fwd_send.at[e], fwd_recv.at[e], mate, rep
        )

    def cut_copy(e):
        here = weights.at[1, 0, cut]
        return remote(here, here, wg_send.at[e], wg_recv.at[e], cut_peer(e), rep)

    def cut_forward(e):
        index = ((cut_out + slice_outer - e) % slice_outer) * 2 + s_in
        there = weights.at[1, 0, index]
        return remote(there, there, wf_send.at[e], wf_recv.at[e], mate, rep)

    for e in range(1, outer):
        pack_copy(e).start()
    fwd_copy(0).start()
    wx.wait_recv()
    for e in range(1, slice_outer):
        cut_copy(e).start()

    def members(i, e):
        same = gid_col == packets[i, e, tiles:tiles + 1, :tiles]
        row = lax.broadcasted_iota(jnp.int32, (tiles + EXTRA, tiles), 0)
        return jnp.where(same | (row >= tiles), 1.0, 0.0).astype(jnp.float32)

    def gathered(i, e):
        m = members(i, e)
        part = jnp.dot(
            m, packets[i, e, :tiles, :],
            precision=lax.Precision.HIGHEST, preferred_element_type=jnp.float32,
        )
        return part, jnp.sum(m, axis=1, keepdims=True)

    total, count = gathered(0, 0)
    for e in range(1, outer):
        pack_copy(e).wait_recv()
        fwd_copy(e).start()
        part, number = gathered(0, e)
        total, count = total + part, count + number
    cut_forward(0).start()
    for e in range(1, slice_outer):
        cut_copy(e).wait_recv()
        cut_forward(e).start()
    for e in range(outer):
        fwd_copy(e).wait_recv()
        part, number = gathered(1, e)
        total, count = total + part, count + number

    row_count = float(local_rows * shuf_size)
    overall = total[tiles:tiles + 1] / row_count
    weight_sum = count[:tiles] * float(tile_rows) + float(PRIOR)
    pooled = (total[:tiles] + float(PRIOR) * overall) / weight_sum
    center, second = pooled[:, :cols], pooled[:, cols:]
    scale = lax.rsqrt(second - center * center + EPS) * gain[...]
    stat[0] = scale
    stat[1] = bias[...] - center * scale

    def stat_copy(dl):
        peer = rep_peer(1, dl)
        rows = pl.ds(pl.multiple_of(peer * block_tiles, 8), stats_in.shape[2])
        return remote(
            stat.at[:, rows], stats_in.at[dl], st_send.at[dl], st_recv.at[dl], shuf, peer
        )

    for dh, dl in far:
        stat_copy(dl).start()

    def scored(block, tile):
        x = held[held_rows(block, tile, 1), :].astype(jnp.float32)
        at = pl.ds(block * block_tiles + tile, 1)
        return (x * stat[0, at, :] + stat[1, at, :]).astype(jnp.bfloat16)

    def late(tile):
        for dh, dl in far:
            peer = rep_peer(dh, dl)
            held[held_rows(peer, tile, 1), :] = scored(peer, tile)
            far_copy(dl, tile).start()

    def late_step(tile, carry):
        late(tile)
        return carry

    lax.fori_loop(early, main_tiles, late_step, 0)
    for tile in range(main_tiles, block_tiles):
        late(tile)

    def near_step(tile, carry):
        for dh, dl in near:
            peer = rep_peer(dh, dl)
            held[held_rows(peer, tile, 1), :] = scored(peer, tile)
        return carry

    lax.fori_loop(0, block_tiles, near_step, 0)
    for dh, dl in near:
        for part in range(2):
            near_copy(dl, part).start()

    def own_step(tile, carry):
        dst, rows = tile_at(tile)
        dst[rows, :cols] = scored(rep, tile)
        return carry

    lax.fori_loop(0, main_tiles, own_step, 0)
    for tile in range(main_tiles, block_tiles):
        own_step(tile, 0)

    own_weight.wait()
    for e in range(slice_outer):
        cut_forward(e).wait_recv()

    def share_copy(dh, dl):
        return remote(
            weights.at[dh, 0], weights.at[dh, dl],
            wn_send.at[dh, dl], wn_recv.at[dh, dl], shuf, rep_peer(0, dl),
        )

    for dl in range(1, half):
        for dh in range(2):
            share_copy(dh, dl).start()
    for dh, dl in far:
        stat_copy(dl).wait_recv()

    def early_step(tile, carry):
        dst, rows = tile_at(tile)
        for dh, dl in far:
            far_copy(dl, tile).wait_recv()
            at = slot_cols(dh, dl)
            x = dst[rows, at].astype(jnp.float32)
            s = stats_in[dl, 0, pl.ds(tile, 1), :]
            t = stats_in[dl, 1, pl.ds(tile, 1), :]
            dst[rows, at] = (x * s + t).astype(jnp.bfloat16)
        return carry

    lax.fori_loop(0, early, early_step, 0)
    for dl in range(1, half):
        for dh in range(2):
            share_copy(dh, dl).wait_recv()
    for dh, dl in near:
        for part in range(2):
            near_copy(dl, part).wait_recv()

    def project(pair, carry):
        for u in range(PAIR):
            tile = pair * PAIR + u

            @pl.when(tile >= early)
            def _():
                for dh, dl in far:
                    far_copy(dl, tile).wait_recv()

        size = PAIR * tile_rows
        rows = pl.ds(pl.multiple_of(pair * size, size), size)
        whole = weights[...].reshape(rep_size * cols, weights.shape[-1])
        out[rows, :] = jnp.dot(
            main[rows, :], whole, preferred_element_type=jnp.float32
        ).astype(out.dtype)
        return carry

    lax.fori_loop(0, main_tiles // PAIR, project, 0)

    wx.wait_send()
    for e in range(1, outer):
        pack_copy(e).wait_send()
    for e in range(outer):
        fwd_copy(e).wait_send()
    for e in range(1, slice_outer):
        cut_copy(e).wait_send()
    for e in range(slice_outer):
        cut_forward(e).wait_send()
    for dh, dl in far:
        stat_copy(dl).wait_send()
    for dl in range(1, half):
        for dh in range(2):
            share_copy(dh, dl).wait_send()
    for dh, dl in near:
        for part in range(2):
            near_copy(dl, part).wait_send()
    for tile in range(block_tiles):
        for dh, dl in far:
            far_copy(dl, tile).wait_send()
    for tile in range(main_tiles, block_tiles):
        for dh, dl in far:
            far_copy(dl, tile).wait_recv()


def finish(early, scored, weights, out, tail, sems):
    rows, size = early.shape[0], scored.shape[0]
    count = rows // size

    def early_copy(i):
        return pltpu.make_async_copy(
            early.at[pl.ds(i * size, size)], out.at[pl.ds(i * size, size)], sems.at[i]
        )

    for i in range(count):
        early_copy(i).start()
    whole = weights[...].reshape(scored.shape[1], weights.shape[-1])
    tail[...] = jnp.dot(scored[...], whole, preferred_element_type=jnp.float32).astype(tail.dtype)
    tail_copy = pltpu.make_async_copy(tail, out.at[pl.ds(rows, size)], sems.at[count])
    tail_copy.start()
    for i in range(count):
        early_copy(i).wait()
    tail_copy.wait()


def on_device(shuf_size, rep_size, values, subgroup, owners, col_gain, col_bias, out_weight):
    local_rows, cols = values.shape
    tiles = subgroup.shape[0]
    outs = out_weight.shape[1]
    slices = math.gcd(shuf_size, cols // 32)
    outer, half, slice_outer = shuf_size // 2, rep_size // 2, slices // 2
    block_rows = local_rows // rep_size
    block_tiles = tiles // rep_size
    final = PAIR * local_rows // tiles
    early = block_tiles * EARLY // 16
    f32, bf16 = jnp.float32, jnp.bfloat16
    dma = pltpu.SemaphoreType.DMA
    vmem = pl.BlockSpec(memory_space=pltpu.VMEM)
    hbm = pl.BlockSpec(memory_space=pltpu.HBM)
    first, last, weights = pl.pallas_call(
        functools.partial(kernel, shuf_size, rep_size, early),
        out_shape=(
            pltpu.VMEM((block_rows - final, outs), bf16),
            pltpu.VMEM((final, rep_size * cols), bf16),
            pltpu.VMEM((2, half, slices, cols // slices, outs), bf16),
        ),
        in_specs=[hbm, hbm, vmem, vmem, vmem, vmem],
        out_specs=(vmem, vmem, vmem),
        scratch_shapes=[
            pltpu.VMEM((local_rows, cols), bf16),
            pltpu.VMEM((block_rows - final, rep_size * cols), bf16),
            pltpu.VMEM((2, outer, tiles + EXTRA, 2 * cols), f32),
            pltpu.VMEM((2, tiles, cols), f32),
            pltpu.VMEM((half, 2, -(-early // 8) * 8, cols), f32),
            pltpu.SemaphoreType.REGULAR,
            pltpu.SemaphoreType.REGULAR,
            dma((rep_size, len(PARTS))),
            dma,
            dma((half, block_tiles)),
            dma((half, block_tiles)),
            dma((half, 2)),
            dma((half, 2)),
            dma((outer,)),
            dma((outer,)),
            dma((outer,)),
            dma((outer,)),
            dma,
            dma,
            dma((slice_outer,)),
            dma((slice_outer,)),
            dma((slice_outer,)),
            dma((slice_outer,)),
            dma((2, half)),
            dma((2, half)),
            dma((half,)),
            dma((half,)),
        ],
        compiler_params=pltpu.CompilerParams(
            collective_id=0, has_side_effects=True, vmem_limit_bytes=LIMIT
        ),
    )(
        values,
        out_weight.reshape(slices, cols // slices, outs),
        owners.reshape(1, tiles),
        subgroup.reshape(1, tiles),
        col_gain[None, :],
        col_bias[None, :],
    )
    return pl.pallas_call(
        finish,
        out_shape=jax.ShapeDtypeStruct((block_rows, outs), bf16),
        in_specs=[vmem, vmem, vmem],
        out_specs=hbm,
        scratch_shapes=[pltpu.VMEM((final, outs), bf16), dma((block_rows // final,))],
        compiler_params=pltpu.CompilerParams(vmem_limit_bytes=LIMIT_LAST),
    )(first, last, weights)


def solution(mesh):
    return jax.shard_map(
        functools.partial(on_device, mesh.shape["shuf"], mesh.shape["rep"]),
        mesh=mesh,
        in_specs=(P("shuf", "rep"), P("shuf"), P("shuf", None), P("rep"), P("rep"), P("rep", None)),
        out_specs=P(("shuf", "rep"), None),
        check_vma=False,
    )
```

time: 56.3 us -> 59.6 us (1.059); the launches traced: 55.4 us -> 59.5 us
  Pallas kernels: 55.4 us -> 59.5 us
    pallas_call x1, Pallas kernels: 53.3 us -> 57.4 us  [on_device(): pl.pallas_call(functools.partial(kernel, shuf_size, rep_size, early), out...]
where the time goes in v1:
time: 59.6 us; the launch traced here: 59.5 us
  Pallas kernels  59.5 us (100%)
    pallas_call x1, Pallas kernels, on_device(): pl.pallas_call(functools.partial(kernel, shuf_size, rep_size, early), out...  57.4 us
    pallas_call x1, Pallas kernels, on_device(): pl.pallas_call(finish, out_shape=jax.ShapeDtypeStruct((block_rows, outs),...  2.07 us

profile of v1, /device:TPU:25, one launch (start us, length us, event | category | flops | bytes accessed | tf_op | source)
XLA Modules:
  0.0 59.5 jit_solution(3368004593632167209)
XLA Ops:
  0.0 57.4 %shard_map.64 = (bf16[1792,1024]{1,0:T(8,128)(2,1)S(1)}, bf16[256,1024]{1,0:T(8,128)(2,1)S(1)}, bf16[2,2,8,32,1024]{4,3,2,1,0:T(8,128)(2,1)S(1)}) custom-call(bf16[8192,256]{1,0:T(8,128)(2,1)} %values.1, bf16[8,32,1024]{2,1,0:T(8,128)(2,1)} %bitcast.5, s32[1,64]{1,0:T(1,128)} %bitcast.8, s32[1,64]{1,0:T(1,128)} %bitcast.9, f32[1,256]{1,0:T(1,128)} %bitcast.6, ...), custom_call_target="tpu_custom_call" | custom-call | tf_op jit(solution)/shard_map/pallas_call | solution.py:450
  57.4 2.1 %shard_map.65 = bf16[2048,1024]{1,0:T(8,128)(2,1)} custom-call(bf16[1792,1024]{1,0:T(8,128)(2,1)S(1)} %get-tuple-element.8.early, bf16[256,1024]{1,0:T(8,128)(2,1)S(1)} %get-tuple-element.9.scored, bf16[2,2,8,32,1024]{4,3,2,1,0:T(8,128)(2,1)S(1)} %get-tuple-element.10.weights), custom_call_target="tpu_custom_call" | custom-call | tf_op jit(solution)/shard_map/pallas_call | solution.py:499

commit v2 on v1

--- a/solution.py
+++ b/solution.py
@@ -26,30 +26,41 @@
     early,
     values,
     weight,
-    owner,
-    member,
-    gain,
-    bias,
+    owner_hbm,
+    member_hbm,
+    gain_hbm,
+    bias_hbm,
     out,
     last,
     weights,
     held,
     main,
     packets,
+    spreads,
+    owner,
+    member,
+    gain,
+    bias,
     stat,
+    stats_out,
     stats_in,
     rep_ready,
     shuf_ready,
     load_sem,
     own_sem,
+    small_sem,
     far_send,
     far_recv,
     near_send,
     near_recv,
     pack_send,
     pack_recv,
+    spread_send,
+    spread_recv,
     fwd_send,
     fwd_recv,
+    over_send,
+    over_recv,
     wx_send,
     wx_recv,
     wg_send,
@@ -139,10 +150,6 @@
     own_weight = pltpu.make_async_copy(weight, weights.at[0, 0], own_sem)
     loads = [(b, i) for i in range(2) for b in range(half)]
     loads += [(b, i) for b in range(rep_size) for i in range(3) if (b, i) not in loads]
-    for b, i in loads:
-        load_copy(b, i).start()
-    own_weight.start()
-
     barrier = pltpu.get_barrier_semaphore()
     leader, scout = low == half - 1, low == 0
     for dh, dl in rep_offsets:
@@ -151,6 +158,18 @@
         @pl.when(peer % half == half - 1)
         def _():
             pl.semaphore_signal(barrier, inc=1, device_id=(shuf, peer), device_id_type=MESH)
+
+    for b, i in loads:
+        load_copy(b, i).start()
+    small = [
+        pltpu.make_async_copy(src, dst, small_sem.at[i])
+        for i, (src, dst) in enumerate(
+            [(owner_hbm, owner), (member_hbm, member), (gain_hbm, gain), (bias_hbm, bias)]
+        )
+    ]
+    for copy in small:
+        copy.start()
+    own_weight.start()
 
     @pl.when(leader)
     def _():
@@ -200,6 +219,8 @@
     def _():
         pl.semaphore_wait(shuf_ready, 1)
 
+    for copy in small:
+        copy.wait()
     gid_row = (owner[...] * GRP_DEV + member[...]).astype(jnp.float32)
     packets[0, 0, tiles:tiles + 1, :tiles] = gid_row
     square = (tiles, tiles)
@@ -209,6 +230,7 @@
     group = 8
     for b in range(rep_size):
         block = rep_peer(*order[b])
+        spread_rows = []
         for g in range(block_tiles // group):
             for i in range(len(PARTS)):
                 if starts[i] < (g + 1) * group:
@@ -219,18 +241,34 @@
                 parts.append(jnp.sum(x, axis=0, keepdims=True))
                 squares.append(jnp.sum(x * x, axis=0, keepdims=True))
             first = pl.multiple_of(block * block_tiles + g * group, group)
-            packets[0, 0, pl.ds(first, group), :cols] = jnp.concatenate(parts, axis=0)
-            packets[0, 0, pl.ds(first, group), cols:] = jnp.concatenate(squares, axis=0)
-
-    def pack_copy(e):
-        return remote(
-            packets.at[0, 0], packets.at[0, e], pack_send.at[e], pack_recv.at[e], outer_peer(e), rep
-        )
-
-    def fwd_copy(e):
-        return remote(
-            packets.at[0, e], packets.at[1, e], fwd_send.at[e], fwd_recv.at[e], mate, rep
-        )
+            part = jnp.concatenate(parts, axis=0)
+            spread = jnp.concatenate(squares, axis=0) - part * part * (1.0 / tile_rows)
+            packets[0, 0, pl.ds(first, group), :] = part
+            spread_rows.append(spread.astype(jnp.bfloat16))
+        at = pl.ds(pl.multiple_of(block * block_tiles, block_tiles), block_tiles)
+        spreads[0, 0, at, :] = jnp.concatenate(spread_rows, axis=0)
+
+    def pack_copies(e):
+        to = outer_peer(e), rep
+        return [
+            remote(packets.at[0, 0], packets.at[0, e], pack_send.at[e], pack_recv.at[e], *to),
+            remote(spreads.at[0, 0], spreads.at[0, e], spread_send.at[e], spread_recv.at[e], *to),
+        ]
+
+    def fwd_copies(e):
+        to = mate, rep
+        return [
+            remote(packets.at[0, e], packets.at[1, e], fwd_send.at[e], fwd_recv.at[e], *to),
+            remote(spreads.at[0, e], spreads.at[1, e], over_send.at[e], over_recv.at[e], *to),
+        ]
+
+    def start(copies):
+        for copy in copies:
+            copy.start()
+
+    def received(copies):
+        for copy in copies:
+            copy.wait_recv()
 
     def cut_copy(e):
         here = weights.at[1, 0, cut]
@@ -242,11 +280,8 @@
         return remote(there, there, wf_send.at[e], wf_recv.at[e], mate, rep)
 
     for e in range(1, outer):
-        pack_copy(e).start()
-    fwd_copy(0).start()
-    wx.wait_recv()
-    for e in range(1, slice_outer):
-        cut_copy(e).start()
+        start(pack_copies(e))
+    start(fwd_copies(0))
 
     def members(i, e):
         same = gid_col == packets[i, e, tiles:tiles + 1, :tiles]
@@ -255,24 +290,26 @@
 
     def gathered(i, e):
         m = members(i, e)
+        sums = packets[i, e, :tiles, :]
+        squares = spreads[i, e].astype(jnp.float32) + sums * sums * (1.0 / tile_rows)
         part = jnp.dot(
-            m, packets[i, e, :tiles, :],
+            m, jnp.concatenate([sums, squares], axis=1),
             precision=lax.Precision.HIGHEST, preferred_element_type=jnp.float32,
         )
         return part, jnp.sum(m, axis=1, keepdims=True)
 
     total, count = gathered(0, 0)
     for e in range(1, outer):
-        pack_copy(e).wait_recv()
-        fwd_copy(e).start()
+        received(pack_copies(e))
+        start(fwd_copies(e))
         part, number = gathered(0, e)
         total, count = total + part, count + number
+    wx.wait_recv()
+    for e in range(1, slice_outer):
+        cut_copy(e).start()
     cut_forward(0).start()
-    for e in range(1, slice_outer):
-        cut_copy(e).wait_recv()
-        cut_forward(e).start()
     for e in range(outer):
-        fwd_copy(e).wait_recv()
+        received(fwd_copies(e))
         part, number = gathered(1, e)
         total, count = total + part, count + number
 
@@ -286,13 +323,14 @@
     stat[1] = bias[...] - center * scale
 
     def stat_copy(dl):
-        peer = rep_peer(1, dl)
-        rows = pl.ds(pl.multiple_of(peer * block_tiles, 8), stats_in.shape[2])
         return remote(
-            stat.at[:, rows], stats_in.at[dl], st_send.at[dl], st_recv.at[dl], shuf, peer
+            stats_out.at[dl], stats_in.at[dl], st_send.at[dl], st_recv.at[dl], shuf, rep_peer(1, dl)
         )
 
     for dh, dl in far:
+        at = pl.ds(pl.multiple_of(rep_peer(dh, dl) * block_tiles, block_tiles), block_tiles)
+        for k in range(2):
+            stats_out[dl, k * early:(k + 1) * early, :] = stat[k, at, :][:early]
         stat_copy(dl).start()
 
     def scored(block, tile):
@@ -313,6 +351,10 @@
     lax.fori_loop(early, main_tiles, late_step, 0)
     for tile in range(main_tiles, block_tiles):
         late(tile)
+
+    for e in range(1, slice_outer):
+        cut_copy(e).wait_recv()
+        cut_forward(e).start()
 
     def near_step(tile, carry):
         for dh, dl in near:
@@ -356,8 +398,8 @@
             far_copy(dl, tile).wait_recv()
             at = slot_cols(dh, dl)
             x = dst[rows, at].astype(jnp.float32)
-            s = stats_in[dl, 0, pl.ds(tile, 1), :]
-            t = stats_in[dl, 1, pl.ds(tile, 1), :]
+            s = stats_in[dl, pl.ds(tile, 1), :]
+            t = stats_in[dl, pl.ds(early + tile, 1), :]
             dst[rows, at] = (x * s + t).astype(jnp.bfloat16)
         return carry
 
@@ -390,9 +432,11 @@
 
     wx.wait_send()
     for e in range(1, outer):
-        pack_copy(e).wait_send()
+        for copy in pack_copies(e):
+            copy.wait_send()
     for e in range(outer):
-        fwd_copy(e).wait_send()
+        for copy in fwd_copies(e):
+            copy.wait_send()
     for e in range(1, slice_outer):
         cut_copy(e).wait_send()
     for e in range(slice_outer):
@@ -454,22 +498,33 @@
             pltpu.VMEM((final, rep_size * cols), bf16),
             pltpu.VMEM((2, half, slices, cols // slices, outs), bf16),
         ),
-        in_specs=[hbm, hbm, vmem, vmem, vmem, vmem],
+        in_specs=[hbm] * 6,
         out_specs=(vmem, vmem, vmem),
         scratch_shapes=[
             pltpu.VMEM((local_rows, cols), bf16),
             pltpu.VMEM((block_rows - final, rep_size * cols), bf16),
-            pltpu.VMEM((2, outer, tiles + EXTRA, 2 * cols), f32),
+            pltpu.VMEM((2, outer, tiles + EXTRA, cols), f32),
+            pltpu.VMEM((2, outer, tiles, cols), bf16),
+            pltpu.VMEM((1, tiles), jnp.int32),
+            pltpu.VMEM((1, tiles), jnp.int32),
+            pltpu.VMEM((1, cols), f32),
+            pltpu.VMEM((1, cols), f32),
             pltpu.VMEM((2, tiles, cols), f32),
-            pltpu.VMEM((half, 2, -(-early // 8) * 8, cols), f32),
+            pltpu.VMEM((half, -(-2 * early // 8) * 8, cols), f32),
+            pltpu.VMEM((half, -(-2 * early // 8) * 8, cols), f32),
             pltpu.SemaphoreType.REGULAR,
             pltpu.SemaphoreType.REGULAR,
             dma((rep_size, len(PARTS))),
             dma,
+            dma((4,)),
             dma((half, block_tiles)),
             dma((half, block_tiles)),
             dma((half, 2)),
             dma((half, 2)),
+            dma((outer,)),
+            dma((outer,)),
+            dma((outer,)),
+            dma((outer,)),
             dma((outer,)),
             dma((outer,)),
             dma((outer,)),

time: 59.6 us -> 54.6 us (0.916); the launches traced: 59.5 us -> 53.7 us
  Pallas kernels: 59.5 us -> 53.7 us
    pallas_call x1, Pallas kernels: 57.4 us -> 51.6 us  [on_device(): pl.pallas_call(functools.partial(kernel, shuf_size, rep_size, early), out...]
where the time goes in v2:
time: 54.6 us; the launch traced here: 53.7 us
  Pallas kernels  53.7 us (98%)
    pallas_call x1, Pallas kernels, on_device(): pl.pallas_call(functools.partial(kernel, shuf_size, rep_size, early), out...  51.6 us
    pallas_call x1, Pallas kernels, on_device(): pl.pallas_call(finish, out_shape=jax.ShapeDtypeStruct((block_rows, outs),...  2.07 us

profile of v2, /device:TPU:25, one launch (start us, length us, event | category | flops | bytes accessed | tf_op | source)
XLA Modules:
  0.0 53.7 jit_solution(1697126810987616138)
XLA Ops:
  0.0 51.6 %shard_map.64 = (bf16[1792,1024]{1,0:T(8,128)(2,1)S(1)}, bf16[256,1024]{1,0:T(8,128)(2,1)S(1)}, bf16[2,2,8,32,1024]{4,3,2,1,0:T(8,128)(2,1)S(1)}) custom-call(bf16[8192,256]{1,0:T(8,128)(2,1)} %values.1, bf16[8,32,1024]{2,1,0:T(8,128)(2,1)} %bitcast.5, s32[1,64]{1,0:T(1,128)} %bitcast.8, s32[1,64]{1,0:T(1,128)} %bitcast.9, f32[1,256]{1,0:T(1,128)} %bitcast.6, ...), custom_call_target="tpu_custom_call" | custom-call | tf_op jit(solution)/shard_map/pallas_call | solution.py:494
  51.6 2.1 %shard_map.65 = bf16[2048,1024]{1,0:T(8,128)(2,1)} custom-call(bf16[1792,1024]{1,0:T(8,128)(2,1)S(1)} %get-tuple-element.8.early, bf16[256,1024]{1,0:T(8,128)(2,1)S(1)} %get-tuple-element.9.scored, bf16[2,2,8,32,1024]{4,3,2,1,0:T(8,128)(2,1)S(1)} %get-tuple-element.10.weights), custom_call_target="tpu_custom_call" | custom-call | tf_op jit(solution)/shard_map/pallas_call | solution.py:554
